TPU v7x, 128 devices: a whole 4x4x4 slice. The times are simulated.
128 devices in a mesh: zero: 32 (over y, x, core), width: 4 (over z).
Axes of the slice: x: 4, y: 4, z: 4, core: 2. Of those that a mesh axis runs over, the one named last changes fastest.
Arguments:
- train_query: bfloat16 [3584, 4096], P('zero', 'width'), may hold values from -0.09375 to 0.09375
- low_query: bfloat16 [3584, 32], P('zero'), may hold values from -0.09375 to 0.09375
- high_query: bfloat16 [32, 4096], P(None, 'width'), may hold values from -1 to 1
- train_key: bfloat16 [3584, 2048], P('zero', 'width'), may hold values from -0.09375 to 0.09375
- low_key: bfloat16 [3584, 32], P('zero'), may hold values from -0.09375 to 0.09375
- high_key: bfloat16 [32, 2048], P(None, 'width'), may hold values from -1 to 1
- train_value: bfloat16 [3584, 2048], P('zero', 'width'), may hold values from -0.09375 to 0.09375
- low_value: bfloat16 [3584, 32], P('zero'), may hold values from -0.09375 to 0.09375
- high_value: bfloat16 [32, 2048], P(None, 'width'), may hold values from -1 to 1
- train_mixed: bfloat16 [4096, 3584], P('width', 'zero'), may hold values from -0.09375 to 0.09375
- low_mixed: bfloat16 [4096, 32], P('width'), may hold values from -0.09375 to 0.09375
- high_mixed: bfloat16 [32, 3584], P(None, 'zero'), may hold values from -1 to 1
- norm_train: float32 [3584], P(('zero', 'width')), may hold values from 0.25 to 1.75
- norm_step: float32 [3584], P(('zero', 'width')), may hold values from -0.3 to 0.3
Outputs:
- ready_query: bfloat16 [4096, 3584], P('width')
- ready_key: bfloat16 [2048, 3584], P('width')
- ready_value: bfloat16 [2048, 3584], P('width')
- ready_mixed: bfloat16 [3584, 4096], P(None, 'width')
- serve_norm: bfloat16 [3584], replicated
All inputs are finite; a program needn't handle non-finite values.
Results may differ from a plain program's by a relative error of at most 0.001.
Values may be sent and summed in bfloat16 or wider, within the bound.
No kernel may reach another device: no remote copies, remote signals or barrier semaphores. Data moves between devices by JAX's collectives and lax.ppermute only.
A program may use at most 128 MiB of HBM per device.

v0:
```python
import jax
import jax.numpy as jnp
from jax import lax
from jax.sharding import Mesh
from jax.sharding import PartitionSpec as P

ZERO = ("zero_0", "zero_1", "zero_2")
ZERO_WIDTH = ("zero_0", "zero_1", "zero_2", "width")
mix_rate = 0.5


def turned_gather(arrays, axis, dims):
    turned = [jnp.moveaxis(a, dim, 0) for a, dim in zip(arrays, dims)]
    both = jnp.concatenate([t.reshape(len(t), -1) for t in turned], axis=1)
    whole, at, done = (lax.all_gather(both, axis, axis=0, tiled=True), 0, [])
    for t, dim in zip(turned, dims):
        piece = whole[:, at : at + t[0].size].reshape(-1, *t.shape[1:])
        done.append(jnp.moveaxis(piece, 0, dim))
        at += t[0].size
    return tuple(done)


def joined_along(pieces, dim):
    lengths = list(pieces.shape[1:])
    lengths[dim] *= pieces.shape[0]
    return jnp.moveaxis(pieces, 0, dim).reshape(lengths)


def gather_in_order(array, axes, sequence):
    pieces = array
    for k in sequence:
        pieces = lax.all_gather(pieces, axes[k])
    done = sequence[::-1]
    back = [done.index(k) for k in range(len(axes))]
    pieces = pieces.transpose(*back, *range(len(axes), pieces.ndim))
    return pieces.reshape(-1, *array.shape)


def gathered_by_axis(array, axes, sequence, dim):
    return joined_along(gather_in_order(array, axes, sequence), dim)


def body(
    train_query,
    low_query,
    high_query,
    train_key,
    low_key,
    high_key,
    train_value,
    low_value,
    high_value,
    train_mixed,
    low_mixed,
    high_mixed,
    norm_train,
    norm_step,
):
    latest_query = train_query.astype(jnp.float32) + mix_rate * jnp.dot(
        low_query, high_query, preferred_element_type=jnp.float32
    )
    latest_key = train_key.astype(jnp.float32) + mix_rate * jnp.dot(
        low_key, high_key, preferred_element_type=jnp.float32
    )
    latest_value = train_value.astype(jnp.float32) + mix_rate * jnp.dot(
        low_value, high_value, preferred_element_type=jnp.float32
    )
    latest_mixed = train_mixed.astype(jnp.float32) + mix_rate * jnp.dot(
        low_mixed, high_mixed, preferred_element_type=jnp.float32
    )
    narrow_query, narrow_key, narrow_value, narrow_mixed = (
        latest_query.astype(jnp.bfloat16),
        latest_key.astype(jnp.bfloat16),
        latest_value.astype(jnp.bfloat16),
        latest_mixed.astype(jnp.bfloat16),
    )
    ready_query, ready_key, ready_value, ready_mixed = turned_gather(
        (narrow_query, narrow_key, narrow_value, narrow_mixed), ZERO, (0, 0, 0, 1)
    )
    ready_query, ready_key, ready_value, ready_mixed = (
        ready_query.T,
        ready_key.T,
        ready_value.T,
        ready_mixed.T,
    )
    serve_norm = gathered_by_axis(
        (norm_train + norm_step).astype(jnp.bfloat16), ZERO_WIDTH, (0, 1, 3, 2), 0
    )
    return (ready_query, ready_key, ready_value, ready_mixed, serve_norm)


def solution(mesh):
    torus = Mesh(
        mesh.devices.reshape(4, 4, 2, mesh.shape["width"]), ("zero_0", "zero_1", "zero_2", "width")
    )
    return jax.shard_map(
        body,
        mesh=torus,
        in_specs=(
            P(ZERO, "width"),
            P(ZERO, None),
            P(None, "width"),
            P(ZERO, "width"),
            P(ZERO, None),
            P(None, "width"),
            P(ZERO, "width"),
            P(ZERO, None),
            P(None, "width"),
            P("width", ZERO),
            P("width", None),
            P(None, ZERO),
            P(ZERO_WIDTH),
            P(ZERO_WIDTH),
        ),
        out_specs=(P("width", None), P("width", None), P("width", None), P(None, "width"), P()),
        check_vma=False,
    )
```

profile of v0, /device:TPU:1, one launch (start us, length us, event | category | flops | bytes accessed | tf_op | source)
XLA Modules:
  0.0 148.0 jit_solution(1790377427683227908)
XLA Ops:
  7.2 0.0 copy-start
  7.2 0.0 copy-start.3
  7.2 0.0 copy-start.1
  7.2 0.0 copy-start.2
  7.2 0.0 all-gather.7.cloned.1.call-start
  7.3 0.8 copy-done
  8.0 1.2 fusion.3
  9.2 1.2 fusion.4
  10.5 1.1 fusion.7
  11.6 1.1 fusion.8
  12.8 0.9 pad_maximum_fusion
  13.7 0.0 all-gather.7.cloned.1.call-update
  13.7 0.0 copy-done.3
  13.7 0.6 dynamic-slice
  14.9 0.0 copy-done.1
  15.0 0.0 copy-done.2
  15.0 0.2 dynamic-update-slice
  15.2 9.5 %all-reduce = bf16[112]{0:T(256)(128)(2,1)S(1)} all-reduce(bf16[112]{0:T(256)(128)(2,1)S(1)} %dynamic-update-slice), channel_id=2, replica_groups=mesh['zero_0'=4,'zero_1'=4,'zero_2'=2,'width'=4] {'zero_0'}, use_global_device_ids=true, to_apply=%add | all-reduce | flops 112 | bytes 448
  24.8 0.1 reshape.17
  24.8 8.1 %all-gather.4 = bf16[4,4,28]{2,1,0:T(4,128)(2,1)S(1)} all-gather(bf16[1,4,28]{2,1,0:T(4,128)(2,1)S(1)} %reshape.17), channel_id=3, replica_groups=mesh['zero_0'=4,'zero_1'=4,'zero_2'=2,'width'=4] {'zero_1'}, dimensions={0}, use_global_device_ids=true | all-gather | bytes 1120 | tf_op jit(solution)/shard_map/all_gather | solution.py:32
  33.0 11.5 %all-gather.2 = bf16[16,4,28]{2,1,0:T(4,128)(2,1)S(1)} all-gather(bf16[4,4,28]{2,1,0:T(4,128)(2,1)S(1)} %all-gather.4), channel_id=4, replica_groups=mesh['zero_0'=4,'zero_1'=4,'zero_2'=2,'width'=4] {'width'}, dimensions={0}, use_global_device_ids=true | all-gather | bytes 4480 | tf_op jit(solution)/shard_map/all_gather | solution.py:32
  44.4 7.5 %all-gather.3 = bf16[8,4,4,28]{3,2,1,0:T(4,128)(2,1)S(1)} all-gather(bf16[4,4,4,28]{3,2,1,0:T(4,128)(2,1)S(1)} %bitcast.24), channel_id=5, replica_groups=mesh['zero_0'=4,'zero_1'=4,'zero_2'=2,'width'=4] {'zero_2'}, dimensions={0}, use_global_device_ids=true | all-gather | bytes 10752 | tf_op jit(solution)/shard_map/all_gather | solution.py:32
  52.0 0.7 reshape_reshape.3
  52.7 49.3 %all-gather.7.cloned.1.call-done = bf16[3584,3072]{1,0:T(8,128)(2,1)} async-done(((bf16[112,3072]{1,0:T(8,128)(2,1)}), bf16[3584,3072]{1,0:T(8,128)(2,1)}) %all-gather.7.cloned.1.call-update) | async-done | bytes 22020112 | tf_op jit(solution)/shard_map/all_gather | solution.py:15
  102.0 10.7 %fusion.9 = (bf16[3584,1024]{1,0:T(8,128)(2,1)}, bf16[1024,3584]{0,1:T(8,128)(2,1)}) fusion(bf16[3584,3072]{1,0:T(8,128)(2,1)} %all-gather.7.cloned.1.call-done), kind=kLoop, calls=%fused_computation.19 | loop fusion | bytes 29360128 | tf_op jit(solution)/shard_map/slice | solution.py:17
  112.7 9.9 %copy.27 = bf16[1024,3584]{1,0:T(8,128)(2,1)} copy(bf16[1024,3584]{0,1:T(8,128)(2,1)} %get-tuple-element.21) | data formatting | bytes 14680064
  122.6 6.7 %slice_bitcast_fusion.1 = (bf16[512,3584]{0,1:T(8,128)(2,1)}, bf16[512,3584]{0,1:T(8,128)(2,1)}) fusion(bf16[3584,3072]{1,0:T(8,128)(2,1)} %all-gather.7.cloned.1.call-done), kind=kLoop, calls=%fused_computation.1 | loop fusion | bytes 14680064 | tf_op jit(solution)/shard_map/transpose | solution.py:83
  129.3 5.9 %copy.28 = bf16[512,3584]{1,0:T(8,128)(2,1)} copy(bf16[512,3584]{0,1:T(8,128)(2,1)} %get-tuple-element.23) | data formatting | bytes 7340032
  135.2 5.9 %copy.29 = bf16[512,3584]{1,0:T(8,128)(2,1)} copy(bf16[512,3584]{0,1:T(8,128)(2,1)} %get-tuple-element.22) | data formatting | bytes 7340032
  (3 shorter events, 0.0 us)
Async XLA Ops:
  7.2 0.8 copy-start
  7.2 6.5 %copy-start.3 = (u32[128]{0:T(128)S(1)}, u32[128]{0:T(128)}, u32[]{:S(2)}) copy-start(u32[128]{0:T(128)} %constant.16) | copy-start | bytes 1540
  7.2 7.8 %copy-start.1 = (f32[28]{0:T(128)S(1)}, f32[28]{0:T(128)}, u32[]{:S(2)}) copy-start(f32[28]{0:T(128)} %param.26) | copy-start | bytes 340
  7.2 7.8 %copy-start.2 = (f32[28]{0:T(128)S(1)}, f32[28]{0:T(128)}, u32[]{:S(2)}) copy-start(f32[28]{0:T(128)} %param.27) | copy-start | bytes 340
  7.2 94.8 %all-gather.7.cloned.1.call-start = ((), (), s32[]{:S(2)}) async-start(), calls=%async_computation | async-start | bytes 22708224 | tf_op jit(solution)/shard_map/all_gather | solution.py:15
Sparse Core Ops, SparseCore 0:
  13.8 88.1 all-gather.6
where the time goes:
time: 149 us; the launch traced here: 148 us
  waiting for transfers between devices  49.3 us (33%)
  local copies, waits for them, and re-layouts  41.6 us (28%)
  blocking collectives  36.6 us (25%)
  between operations  14.8 us (10%)
  matrix products  4.73 us (3%)
    all_gather x1, waiting for transfers between devices, turned_gather(): whole, at, done = (lax.all_gather(both, axis, axis=0, tiled=True), 0, [])  49.3 us
    all_gather x3, blocking collectives, gather_in_order(): pieces = lax.all_gather(pieces, axes[k])  27.1 us
    unnamed x15, local copies, waits for them, and re-layouts  23.4 us
    slice x1, local copies, waits for them, and re-layouts, turned_gather(): piece = whole[:, at:at + t[0].size].reshape(-1, *t.shape[1:])  10.7 us
    unnamed x1, blocking collectives  9.52 us
    transpose x1, local copies, waits for them, and re-layouts, body(): ready_query, ready_key, ready_value, ready_mixed = (ready_query.T, ready_...  6.68 us
  transfers between devices with their start and end apart: 1, of which 1 were waited for; matrix products, arithmetic and copies ran while one was open for 1% of the time, Pallas kernels for 0%

commit v1 on v0

--- a/solution.py
+++ b/solution.py
@@ -12,7 +12,13 @@
 def turned_gather(arrays, axis, dims):
     turned = [jnp.moveaxis(a, dim, 0) for a, dim in zip(arrays, dims)]
     both = jnp.concatenate([t.reshape(len(t), -1) for t in turned], axis=1)
-    whole, at, done = (lax.all_gather(both, axis, axis=0, tiled=True), 0, [])
+    whole, at, done = (
+        jnp.concatenate(
+            lax.all_to_all(jnp.stack([both] * lax.axis_size(axis)), axis, 0, 0), axis=0
+        ),
+        0,
+        [],
+    )
     for t, dim in zip(turned, dims):
         piece = whole[:, at : at + t[0].size].reshape(-1, *t.shape[1:])
         done.append(jnp.moveaxis(piece, 0, dim))

time: 149 us -> 360 us (2.42)
  blocking collectives: 36.6 us -> 291 us
  waiting for transfers between devices: 49.3 us -> 0.01 us
  between operations: 14.8 us -> 1.39 us
  local copies, waits for them, and re-layouts: 41.6 us -> 50.9 us
  starting transfers between devices: 0.04 us -> 8.76 us
    unnamed x1, blocking collectives: 9.52 us -> 260 us
    all_gather x1 -> x0, waiting for transfers between devices: 49.3 us -> none  [turned_gather(): whole, at, done = (lax.all_gather(both, axis, axis=0, tiled=True), 0, [])]
    another operation x0 -> x1, local copies, waits for them, and re-layouts: none -> 9.21 us  [turned_gather(): jnp.stack([both] * lax.axis_size(axis))]
    all_to_all x0 -> x1, starting transfers between devices: none -> 8.76 us  [turned_gather(): lax.all_to_all(jnp.stack([both] * lax.axis_size(axis)), axis, 0, 0)]
    all_gather x3, blocking collectives: 27.1 us -> 31.4 us  [gather_in_order(): pieces = lax.all_gather(pieces, axes[k])]
    unnamed x15 -> x17, local copies, waits for them, and re-layouts: 23.4 us -> 23.6 us
  transfers between devices with their start and end apart: 1 -> 1, of which waited for: 1 -> 0; matrix products, arithmetic and copies ran while one was open for 1% -> 0% of each run, Pallas kernels for 0% -> 0%
where the time goes in v1:
time: 360 us; the launch traced here: 357 us
  blocking collectives  291 us (81%)
  local copies, waits for them, and re-layouts  50.9 us (14%)
  starting transfers between devices  8.76 us (2%)
  matrix products  4.73 us (1%)
    unnamed x1, blocking collectives  260 us
    all_gather x3, blocking collectives, gather_in_order(): pieces = lax.all_gather(pieces, axes[k])  31.4 us
    unnamed x17, local copies, waits for them, and re-layouts  23.6 us
    slice x1, local copies, waits for them, and re-layouts, turned_gather(): piece = whole[:, at:at + t[0].size].reshape(-1, *t.shape[1:])  10.7 us
    another operation x1, local copies, waits for them, and re-layouts, turned_gather(): jnp.stack([both] * lax.axis_size(axis))  9.21 us
    all_to_all x1, starting transfers between devices, turned_gather(): lax.all_to_all(jnp.stack([both] * lax.axis_size(axis)), axis, 0, 0)  8.76 us
  transfers between devices with their start and end apart: 1, of which 0 were waited for; matrix products, arithmetic and copies ran while one was open for 0% of the time, Pallas kernels for 0%

profile of v1, /device:TPU:1, one launch (start us, length us, event | category | flops | bytes accessed | tf_op | source)
XLA Modules:
  0.0 357.0 jit_solution(13324261744216593564)
XLA Ops:
  0.6 0.0 copy-start
  0.6 0.8 copy-done
  1.5 1.2 fusion.3
  2.7 1.2 fusion.4
  3.9 1.1 fusion.7
  5.1 1.1 fusion.8
  6.2 0.1 pad_maximum_fusion
  6.3 9.2 %stack.2 = bf16[32,112,3072]{2,1,0:T(8,128)(2,1)} broadcast(bf16[112,3072]{1,0:T(8,128)(2,1)S(1)} %pad_maximum_fusion), dimensions={1,2} | broadcast | bytes 22708224 | tf_op jit(solution)/shard_map/stack | solution.py:17
  15.5 0.0 copy-start.4
  15.5 0.0 copy-start.2
  15.5 0.0 copy-start.3
  15.5 8.8 %all-to-all-start = ((bf16[32,112,3072]{2,1,0:T(8,128)(2,1)}), bf16[32,112,3072]{2,1,0:T(8,128)(2,1)}, u32[]{:S(2)}, u32[]{:S(2)}) async-start(bf16[32,112,3072]{2,1,0:T(8,128)(2,1)} %stack.2), calls=%async_computation | async-start | bytes 44040192 | tf_op jit(solution)/shard_map/all_to_all | solution.py:17
  24.3 0.0 copy-done.4
  24.3 0.6 dynamic-slice
  25.5 0.0 copy-done.2
  25.5 0.0 copy-done.3
  25.6 0.2 dynamic-update-slice
  25.8 259.8 %all-reduce = bf16[112]{0:T(256)(128)(2,1)S(1)} all-reduce(bf16[112]{0:T(256)(128)(2,1)S(1)} %dynamic-update-slice), channel_id=2, replica_groups=mesh['zero_0'=4,'zero_1'=4,'zero_2'=2,'width'=4] {'zero_0'}, use_global_device_ids=true, to_apply=%add | all-reduce | flops 112 | bytes 448
  285.6 0.1 reshape.23
  285.7 15.3 %all-gather.4 = bf16[4,4,28]{2,1,0:T(4,128)(2,1)S(1)} all-gather(bf16[1,4,28]{2,1,0:T(4,128)(2,1)S(1)} %reshape.23), channel_id=3, replica_groups=mesh['zero_0'=4,'zero_1'=4,'zero_2'=2,'width'=4] {'zero_1'}, dimensions={0}, use_global_device_ids=true | all-gather | bytes 1120 | tf_op jit(solution)/shard_map/all_gather | solution.py:38
  301.0 10.3 %all-gather.2 = bf16[16,4,28]{2,1,0:T(4,128)(2,1)S(1)} all-gather(bf16[4,4,28]{2,1,0:T(4,128)(2,1)S(1)} %all-gather.4), channel_id=4, replica_groups=mesh['zero_0'=4,'zero_1'=4,'zero_2'=2,'width'=4] {'width'}, dimensions={0}, use_global_device_ids=true | all-gather | bytes 4480 | tf_op jit(solution)/shard_map/all_gather | solution.py:38
  311.3 5.8 %all-gather.3 = bf16[8,4,4,28]{3,2,1,0:T(4,128)(2,1)S(1)} all-gather(bf16[4,4,4,28]{3,2,1,0:T(4,128)(2,1)S(1)} %bitcast.25), channel_id=5, replica_groups=mesh['zero_0'=4,'zero_1'=4,'zero_2'=2,'width'=4] {'zero_2'}, dimensions={0}, use_global_device_ids=true | all-gather | bytes 10752 | tf_op jit(solution)/shard_map/all_gather | solution.py:38
  317.1 0.7 reshape_reshape.3
  317.8 0.0 all-to-all-done
  317.8 10.7 %fusion.9 = (bf16[3584,1024]{1,0:T(8,128)(2,1)}, bf16[1024,3584]{0,1:T(8,128)(2,1)}) fusion(bf16[3584,3072]{1,0:T(8,128)(2,1)} %bitcast.1), kind=kLoop, calls=%fused_computation.19 | loop fusion | bytes 29360128 | tf_op jit(solution)/shard_map/slice | solution.py:23
  328.5 6.7 %slice_bitcast_fusion.1 = (bf16[512,3584]{0,1:T(8,128)(2,1)}, bf16[512,3584]{0,1:T(8,128)(2,1)}) fusion(bf16[3584,3072]{1,0:T(8,128)(2,1)} %bitcast.1), kind=kLoop, calls=%fused_computation.1 | loop fusion | bytes 14680064 | tf_op jit(solution)/shard_map/transpose | solution.py:89
  335.2 9.9 %copy.27 = bf16[1024,3584]{1,0:T(8,128)(2,1)} copy(bf16[1024,3584]{0,1:T(8,128)(2,1)} %get-tuple-element.21) | data formatting | bytes 14680064
  345.2 5.9 %copy.28 = bf16[512,3584]{1,0:T(8,128)(2,1)} copy(bf16[512,3584]{0,1:T(8,128)(2,1)} %get-tuple-element.23) | data formatting | bytes 7340032
  351.1 0.0 copy-start.1
  351.1 5.9 %copy.29 = bf16[512,3584]{1,0:T(8,128)(2,1)} copy(bf16[512,3584]{0,1:T(8,128)(2,1)} %get-tuple-element.22) | data formatting | bytes 7340032
  357.0 0.0 copy-done.1
  (3 shorter events, 0.0 us)
Async XLA Ops:
  0.6 0.8 copy-start
  15.5 8.8 %copy-start.4 = (u32[128]{0:T(128)S(1)}, u32[128]{0:T(128)}, u32[]{:S(2)}) copy-start(u32[128]{0:T(128)} %constant.16) | copy-start | bytes 1540
  15.5 10.0 %copy-start.2 = (f32[28]{0:T(128)S(1)}, f32[28]{0:T(128)}, u32[]{:S(2)}) copy-start(f32[28]{0:T(128)} %param.26) | copy-start | bytes 340
  15.5 10.0 %copy-start.3 = (f32[28]{0:T(128)S(1)}, f32[28]{0:T(128)}, u32[]{:S(2)}) copy-start(f32[28]{0:T(128)} %param.27) | copy-start | bytes 340
  15.5 302.3 %all-to-all-start = ((bf16[32,112,3072]{2,1,0:T(8,128)(2,1)}), bf16[32,112,3072]{2,1,0:T(8,128)(2,1)}, u32[]{:S(2)}, u32[]{:S(2)}) async-start(bf16[32,112,3072]{2,1,0:T(8,128)(2,1)} %stack.2), calls=%async_computation | async-start | bytes 44040192 | tf_op jit(solution)/shard_map/all_to_all | solution.py:17
  351.1 5.9 %copy-start.1 = (bf16[32,1024]{1,0:T(8,128)(2,1)S(1)}, bf16[32,1024]{1,0:T(8,128)(2,1)}, u32[]{:S(2)}) copy-start(bf16[32,1024]{1,0:T(8,128)(2,1)} %param.16) | copy-start | bytes 196612
